TPU v7x, 512 devices: a whole 4x8x8 slice. The times are simulated.
512 devices in a mesh: list: 32 (over y_hi, x, core), shard: 16 (over z, y_lo).
Axes of the slice: x: 4, y: 8 (y_hi: 4, y_lo: 2; y = y_hi * 2 + y_lo), z: 8, core: 2. Of those that a mesh axis runs over, the one named last changes fastest.
Arguments:
- features: bfloat16 [4096, 4096], P(('list', 'shard')), may hold values from -6 to 6
- norm_gain: float32 [4096], replicated, may hold values from 0.5 to 1.5
- gate_weight: bfloat16 [4096, 11008], P('shard', 'list'), may hold values from -0.09375 to 0.09375
- up_weight: bfloat16 [4096, 11008], P('shard', 'list'), may hold values from -0.09375 to 0.09375
- down_weight: bfloat16 [11008, 4096], P('list', 'shard'), may hold values from -0.0546875 to 0.0546875
- centroids: float32 [64, 4096], P('list'), may hold values from -6 to 6
- list_ids: int32 [4096], P(('list', 'shard')), may hold values from 0 to 63
- live: int32 [4096], P(('list', 'shard')), may hold values 0 or 1
Outputs:
- residuals: bfloat16 [4096, 4096], P(('list', 'shard'))
- refreshed: float32 [64, 4096], P('list')
All inputs are finite; a program needn't handle non-finite values. No bound on the sum of `live` on one device may be relied on, other than what follows from the above.
Results may differ from a plain program's by a relative error of at most 0.015.
Values may be sent and summed in bfloat16 or wider, within the bound.
No kernel may reach another device: no remote copies, remote signals or barrier semaphores. Data moves between devices by JAX's collectives and lax.ppermute only.
A program may use at most 64 MiB of HBM per device.

v0:
```python
import jax
import jax.numpy as jnp
from jax import lax
from jax.sharding import PartitionSpec as P


def laid_out(parts, dim):
    shape = list(parts.shape[1:])
    shape[dim] *= parts.shape[0]
    return jnp.moveaxis(parts, 0, dim).reshape(shape)


def from_everyone(value, axis):
    copies = jnp.broadcast_to(value, (lax.axis_size(axis), *value.shape))
    return lax.all_to_all(copies, axis, split_axis=0, concat_axis=0, tiled=True)


def collect(value, axis, dim):
    return laid_out(from_everyone(value, axis), dim)


def in_one_piece(arrays, axis, dim, along):
    both = jnp.concatenate(arrays, axis=along)
    filled, at, done = (lax.all_gather(both, axis, axis=dim, tiled=True), 0, [])
    for a in arrays:
        done.append(lax.slice_in_dim(filled, at, at + a.shape[along], axis=along))
        at += a.shape[along]
    return tuple(done)


def split_up(value, dim, peers):
    before, after = (value.shape[:dim], value.shape[dim + 1 :])
    return jnp.moveaxis(value.reshape(*before, peers, -1, *after), dim, 0)


def sum_at_owner(value, axis, dim):
    peers = lax.axis_size(axis)
    parts = lax.all_to_all(split_up(value, dim, peers), axis, 0, 0, tiled=True)
    return jnp.sum(parts.astype(jnp.float32), axis=0)


def sent_together(arrays, axis, dim, along):
    columns = [a.reshape(*a.shape[:along], -1) for a in arrays]
    both = jnp.concatenate(columns, axis=along)
    filled, at, done = (sum_at_owner(both, axis, dim), 0, [])
    for a, column in zip(arrays, columns):
        share = filled[..., at : at + column.shape[along]]
        done.append(share.reshape(*share.shape[:along], *a.shape[along:]))
        at += column.shape[along]
    return tuple(done)


def taken_together(value, axis):
    return from_everyone(value, axis).astype(jnp.float32).sum(axis=0)


def body(features, norm_gain, gate_weight, up_weight, down_weight, centroids, list_ids, live):
    group_rows = collect(features, "list", 0)
    pieces = in_one_piece((gate_weight, up_weight), "shard", 0, 1)
    first = jnp.dot(group_rows, pieces[0], preferred_element_type=jnp.float32)
    second = jnp.dot(group_rows, pieces[1], preferred_element_type=jnp.float32)
    hidden = (jax.nn.silu(first) * second).astype(jnp.bfloat16)
    partial_sums = jnp.dot(
        hidden,
        lax.all_gather(down_weight, "shard", axis=1, tiled=True),
        preferred_element_type=jnp.float32,
    )
    mixed = sum_at_owner(partial_sums.astype(jnp.bfloat16), "list", 0)
    stream = features.astype(jnp.float32) + mixed
    scale = lax.rsqrt(jnp.mean(stream * stream, axis=1, keepdims=True) + 1e-05)
    embedding = (stream * scale * norm_gain).astype(jnp.bfloat16)
    table = lax.all_gather(centroids.astype(jnp.bfloat16), "list", axis=0, tiled=True)
    list_total = table.shape[0]
    alive = live.astype(jnp.float32)
    member = (list_ids[:, None] == jnp.arange(list_total, dtype=jnp.int32)[None, :]).astype(
        jnp.float32
    )
    picked = jnp.dot(member.astype(jnp.bfloat16), table, preferred_element_type=jnp.float32)
    residuals = (alive[:, None] * (embedding.astype(jnp.float32) - picked)).astype(jnp.bfloat16)
    weighted = member * alive[:, None]
    dense_sums = jnp.dot(weighted.T, embedding.astype(jnp.float32), precision=lax.Precision.HIGHEST)
    dense_counts = jnp.sum(weighted, axis=0)
    owned_sums, owned_counts = sent_together(
        (dense_sums.astype(jnp.bfloat16), dense_counts.astype(jnp.bfloat16)), "list", 0, 1
    )
    total_sums, total_counts = (
        taken_together(owned_sums.astype(jnp.bfloat16), "shard").astype(jnp.float32),
        taken_together(owned_counts.astype(jnp.bfloat16), "shard").astype(jnp.float32),
    )
    refreshed = (centroids + total_sums) / (1.0 + total_counts[:, None])
    return (residuals, refreshed)


def solution(mesh):
    in_specs = (
        P(("list", "shard"), None),
        P(),
        P("shard", "list"),
        P("shard", "list"),
        P("list", "shard"),
        P("list", None),
        P(("list", "shard")),
        P(("list", "shard")),
    )
    out_specs = (P(("list", "shard"), None), P("list", None))
    return jax.shard_map(body, mesh=mesh, in_specs=in_specs, out_specs=out_specs, check_vma=False)
```

profile of v0, /device:TPU:1, one launch (start us, length us, event | category | flops | bytes accessed | tf_op | source)
XLA Modules:
  0.0 452.9 jit_solution(17762954597065309443)
XLA Ops:
  7.2 1.8 pad_maximum_fusion.1
  9.1 0.7 all-gather.6.cloned.1.call-update
  9.8 1.1 broadcast_in_dim.6
  10.9 81.3 %all_to_all.26 = bf16[32,8,4096]{2,1,0:T(8,128)(2,1)S(1)} all-to-all(bf16[32,8,4096]{2,1,0:T(8,128)(2,1)S(1)} %broadcast_in_dim.6), channel_id=1, replica_groups=mesh['list'=32,'shard'=16] {'list'}, dimensions={0} | all-to-all | bytes 4194304 | tf_op jit(solution)/shard_map/all_to_all | solution.py:15
  92.2 94.7 %all-gather.4.cloned.1.call-done = bf16[4096,688]{0,1:T(8,128)(2,1)} async-done(((bf16[256,688]{0,1:T(8,128)(2,1)}), bf16[4096,688]{0,1:T(8,128)(2,1)}) %all-gather.4.cloned.1.call-update) | async-done | bytes 5636112 | tf_op jit(solution)/shard_map/all_gather | solution.py:24
  186.9 2.9 fusion.9
  189.8 77.1 %all-gather.6.cloned.1.call-done = bf16[344,4096]{1,0:T(8,128)(2,1)} async-done(((bf16[344,256]{1,0:T(8,128)(2,1)}), bf16[344,4096]{1,0:T(8,128)(2,1)}) %all-gather.6.cloned.1.call-update) | async-done | bytes 2818064 | tf_op jit(solution)/shard_map/all_gather | solution.py:65
  266.9 7.7 %fusion = bf16[32,8,4096]{2,1,0:T(8,128)(2,1)} fusion(bf16[344,4096]{1,0:T(8,128)(2,1)} %all-gather.6.cloned.1.call-done, bf16[32,8,4096]{2,1,0:T(8,128)(2,1)S(1)} %all_to_all.26, bf16[4096,688]{0,1:T(8,128)(2,1)} %all-gather.4.cloned.1.call-done, f32[256,344]{0,1:T(8,128)S(1)} %fusion.9), kind=kOutput, calls=%fused_computation.1 | convolution fusion | flops 1444417536 | bytes 10182656 | tf_op jit(solution)/shard_map/dot_general | solution.py:63
  274.6 19.3 %all-to-all-start.1 = ((bf16[32,8,4096]{2,1,0:T(8,128)(2,1)}), bf16[32,8,4096]{2,1,0:T(8,128)(2,1)S(1)}, u32[]{:S(2)}, u32[]{:S(2)}) async-start(bf16[32,8,4096]{2,1,0:T(8,128)(2,1)} %fusion), calls=%async_computation.1 | async-start | bytes 4194304 | tf_op jit(solution)/shard_map/all_to_all | solution.py:38
  294.1 0.1 convert_element_type.84
  294.2 50.7 %all-to-all-done.1 = bf16[32,8,4096]{2,1,0:T(8,128)(2,1)S(1)} async-done(((bf16[32,8,4096]{2,1,0:T(8,128)(2,1)}), bf16[32,8,4096]{2,1,0:T(8,128)(2,1)S(1)}, u32[]{:S(2)}, u32[]{:S(2)}) %all-to-all-start.1) | async-done | bytes 2097184 | tf_op jit(solution)/shard_map/all_to_all | solution.py:38
  344.9 0.3 convert_reduce_fusion
  345.2 0.2 multiply_reduce_fusion
  345.5 0.7 convolution_convert_fusion.1
  346.2 0.3 concatenate.10
  346.5 0.5 pad_maximum_fusion
  347.1 23.8 %all_to_all.27 = bf16[32,2,4097]{2,1,0:T(2,128)(2,1)S(1)} all-to-all(bf16[32,2,4097]{2,1,0:T(2,128)(2,1)S(1)} %pad_maximum_fusion), channel_id=1, replica_groups=mesh['list'=32,'shard'=16] {'list'}, dimensions={0} | all-to-all | bytes 1048832 | tf_op jit(solution)/shard_map/all_to_all | solution.py:38
  370.9 0.4 reduce.1
  371.4 0.1 slice_reduce_fusion
  371.5 0.6 broadcast_in_dim.8
  372.1 5.5 %all-to-all-start.4 = ((bf16[16,1,2]{2,1,0:T(2,128)(2,1)}), bf16[16,1,2]{2,1,0:T(2,128)(2,1)S(1)}, u32[]{:S(2)}, u32[]{:S(2)}) async-start(bf16[16,1,2]{2,1,0:T(2,128)(2,1)} %broadcast_in_dim.8), calls=%async_computation.4 | async-start | bytes 16384 | tf_op jit(solution)/shard_map/all_to_all | solution.py:15
  377.6 7.3 %all-to-all-done.4 = bf16[16,1,2]{2,1,0:T(2,128)(2,1)S(1)} async-done(((bf16[16,1,2]{2,1,0:T(2,128)(2,1)}), bf16[16,1,2]{2,1,0:T(2,128)(2,1)S(1)}, u32[]{:S(2)}, u32[]{:S(2)}) %all-to-all-start.4) | async-done | bytes 96 | tf_op jit(solution)/shard_map/all_to_all | solution.py:15
  384.9 0.9 broadcast_in_dim.7
  385.8 3.5 all-to-all-start.3
  389.3 0.1 copy.21
  389.4 0.1 convert_reduce_fusion.2
  389.5 8.6 %all-to-all-done.3 = bf16[16,2,4096]{2,1,0:T(2,128)(2,1)S(1)} async-done(((bf16[16,2,4096]{2,1,0:T(2,128)(2,1)}), bf16[16,2,4096]{2,1,0:T(2,128)(2,1)S(1)}, u32[]{:S(2)}, u32[]{:S(2)}) %all-to-all-start.3) | async-done | bytes 262176 | tf_op jit(solution)/shard_map/all_to_all | solution.py:15
  398.1 0.2 convert_reduce_fusion.1
  398.4 0.7 add_divide_fusion
  399.1 46.0 %all-gather = bf16[32,2,4096]{2,1,0:T(2,128)(2,1)S(1)} all-gather(bf16[1,2,4096]{2,1,0:T(2,128)(2,1)S(1)} %get-tuple-element.3), channel_id=1, replica_groups=mesh['list'=32,'shard'=16] {'list'}, dimensions={0}, use_global_device_ids=true | all-gather | bytes 540672 | tf_op jit(solution)/shard_map/all_gather | solution.py:72
  445.0 0.2 reshape.51
  445.2 0.9 fusion.2
  (19 shorter events, 0.3 us)
Async XLA Ops:
  7.2 179.7 %all-gather.4.cloned.1.call-start = ((), (), s32[]{:S(2)}) async-start(), calls=%async_computation.5 | async-start | bytes 5988352 | tf_op jit(solution)/shard_map/all_gather | solution.py:24
  9.0 257.9 %all-gather.6.cloned.1.call-start = ((), (), s32[]{:S(2)}) async-start(), calls=%async_computation.6 | async-start | bytes 2994176 | tf_op jit(solution)/shard_map/all_gather | solution.py:65
  274.6 19.3 %copy-start.4 = (s32[8]{0:T(128)S(1)}, s32[8]{0:T(128)}, u32[]{:S(2)}) copy-start(s32[8]{0:T(128)} %param.15) | copy-start | bytes 100
  274.6 19.4 %copy-start.3 = (s32[8]{0:T(128)S(1)}, s32[8]{0:T(128)}, u32[]{:S(2)}) copy-start(s32[8]{0:T(128)} %param.14) | copy-start | bytes 100
  274.6 70.6 %copy-start = (bf16[8,4096]{1,0:T(8,128)(2,1)S(1)}, bf16[8,4096]{1,0:T(8,128)(2,1)}, u32[]{:S(2)}) copy-start(bf16[8,4096]{1,0:T(8,128)(2,1)} %param.8) | copy-start | bytes 196612
  274.6 70.8 %copy-start.2 = (f32[4096]{0:T(1024)S(1)}, f32[4096]{0:T(1024)}, u32[]{:S(2)}) copy-start(f32[4096]{0:T(1024)} %param.9) | copy-start | bytes 49156
  274.6 70.3 %all-to-all-start.1 = ((bf16[32,8,4096]{2,1,0:T(8,128)(2,1)}), bf16[32,8,4096]{2,1,0:T(8,128)(2,1)S(1)}, u32[]{:S(2)}, u32[]{:S(2)}) async-start(bf16[32,8,4096]{2,1,0:T(8,128)(2,1)} %fusion), calls=%async_computation.1 | async-start | bytes 4194304 | tf_op jit(solution)/shard_map/all_to_all | solution.py:38
  345.5 52.9 %copy-start.1 = (f32[2,4096]{1,0:T(2,128)S(1)}, f32[2,4096]{1,0:T(2,128)}, u32[]{:S(2)}) copy-start(f32[2,4096]{1,0:T(2,128)} %param.13) | copy-start | bytes 98308
  372.1 12.8 %all-to-all-start.4 = ((bf16[16,1,2]{2,1,0:T(2,128)(2,1)}), bf16[16,1,2]{2,1,0:T(2,128)(2,1)S(1)}, u32[]{:S(2)}, u32[]{:S(2)}) async-start(bf16[16,1,2]{2,1,0:T(2,128)(2,1)} %broadcast_in_dim.8), calls=%async_computation.4 | async-start | bytes 16384 | tf_op jit(solution)/shard_map/all_to_all | solution.py:15
  385.8 12.4 %all-to-all-start.3 = ((bf16[16,2,4096]{2,1,0:T(2,128)(2,1)}), bf16[16,2,4096]{2,1,0:T(2,128)(2,1)S(1)}, u32[]{:S(2)}, u32[]{:S(2)}) async-start(bf16[16,2,4096]{2,1,0:T(2,128)(2,1)} %broadcast_in_dim.7), calls=%async_computation.3 | async-start | bytes 524288 | tf_op jit(solution)/shard_map/all_to_all | solution.py:15
Sparse Core Ops, SparseCore 0:
  10.0 176.8 all-gather.3
  188.9 77.9 all-gather.5
where the time goes:
time: 453 us
  waiting for transfers between devices  239 us (53%)
  blocking collectives  151 us (33%)
  starting transfers between devices  28.4 us (6%)
  between operations  14.2 us (3%)
  matrix products  12.2 us (3%)
    all_gather x1, waiting for transfers between devices, in_one_piece(): filled, at, done = (lax.all_gather(both, axis, axis=dim, tiled=True), 0, [])  94.7 us
    all_to_all x1, blocking collectives, from_everyone(): return lax.all_to_all(copies, axis, split_axis=0, concat_axis=0, tiled=True)  81.3 us
    all_gather x1, waiting for transfers between devices, body(): lax.all_gather(down_weight, 'shard', axis=1, tiled=True)  77.1 us
    all_to_all x1, waiting for transfers between devices, sum_at_owner(): parts = lax.all_to_all(split_up(value, dim, peers), axis, 0, 0, tiled=True)  50.7 us
    all_gather x1, blocking collectives, body(): lax.all_gather(centroids.astype(jnp.bfloat16), 'list', axis=0, tiled=True)  46 us
    all_to_all x1, blocking collectives, sum_at_owner(): parts = lax.all_to_all(split_up(value, dim, peers), axis, 0, 0, tiled=True)  23.8 us
    all_to_all x1, starting transfers between devices, sum_at_owner(): parts = lax.all_to_all(split_up(value, dim, peers), axis, 0, 0, tiled=True)  19.3 us
    all_to_all x2, waiting for transfers between devices, from_everyone(): return lax.all_to_all(copies, axis, split_axis=0, concat_axis=0, tiled=True)  15.9 us
  transfers between devices with their start and end apart: 5, of which 5 were waited for; matrix products, arithmetic and copies ran while one was open for 1% of the time, Pallas kernels for 0%

commit v1 on v0

--- a/solution.py
+++ b/solution.py
@@ -1,7 +1,18 @@
+import functools
 import jax
 import jax.numpy as jnp
 from jax import lax
 from jax.sharding import PartitionSpec as P
+
+
+def _watch_teams(mine_x, dimension_no):
+    oldest = lax.axis_size("list")
+    h_now = jnp.stack([mine_x] * oldest)
+    back = lax.all_to_all(h_now, "list", split_axis=0, concat_axis=0)
+    return jnp.concatenate(back, dimension_no)
+
+
+pack_the_heaps = functools.partial(_watch_teams, dimension_no=0)
 
 
 def laid_out(parts, dim):
@@ -69,7 +80,7 @@
     stream = features.astype(jnp.float32) + mixed
     scale = lax.rsqrt(jnp.mean(stream * stream, axis=1, keepdims=True) + 1e-05)
     embedding = (stream * scale * norm_gain).astype(jnp.bfloat16)
-    table = lax.all_gather(centroids.astype(jnp.bfloat16), "list", axis=0, tiled=True)
+    table = pack_the_heaps(centroids.astype(jnp.bfloat16))
     list_total = table.shape[0]
     alive = live.astype(jnp.float32)
     member = (list_ids[:, None] == jnp.arange(list_total, dtype=jnp.int32)[None, :]).astype(

time: 453 us -> 432 us (0.954)
  blocking collectives: 151 us -> 129 us
    all_gather x1 -> x0, blocking collectives: 46 us -> none  [body(): lax.all_gather(centroids.astype(jnp.bfloat16), 'list', axis=0, tiled=True)]
    all_to_all x0 -> x1, blocking collectives: none -> 24 us  [_watch_teams(): back = lax.all_to_all(h_now, 'list', split_axis=0, concat_axis=0)]
where the time goes in v1:
time: 432 us; the launch traced here: 431 us
  waiting for transfers between devices  239 us (55%)
  blocking collectives  129 us (30%)
  starting transfers between devices  28.4 us (7%)
  between operations  14.2 us (3%)
  matrix products  12.2 us (3%)
  other arithmetic  4.44 us (1%)
    all_gather x1, waiting for transfers between devices, in_one_piece(): filled, at, done = (lax.all_gather(both, axis, axis=dim, tiled=True), 0, [])  94.7 us
    all_to_all x1, blocking collectives, from_everyone(): return lax.all_to_all(copies, axis, split_axis=0, concat_axis=0, tiled=True)  81.3 us
    all_gather x1, waiting for transfers between devices, body(): lax.all_gather(down_weight, 'shard', axis=1, tiled=True)  77.1 us
    all_to_all x1, waiting for transfers between devices, sum_at_owner(): parts = lax.all_to_all(split_up(value, dim, peers), axis, 0, 0, tiled=True)  50.7 us
    all_to_all x1, blocking collectives, _watch_teams(): back = lax.all_to_all(h_now, 'list', split_axis=0, concat_axis=0)  24 us
    all_to_all x1, blocking collectives, sum_at_owner(): parts = lax.all_to_all(split_up(value, dim, peers), axis, 0, 0, tiled=True)  23.8 us
    all_to_all x1, starting transfers between devices, sum_at_owner(): parts = lax.all_to_all(split_up(value, dim, peers), axis, 0, 0, tiled=True)  19.3 us
    all_to_all x2, waiting for transfers between devices, from_everyone(): return lax.all_to_all(copies, axis, split_axis=0, concat_axis=0, tiled=True)  15.9 us
  transfers between devices with their start and end apart: 5, of which 5 were waited for; matrix products, arithmetic and copies ran while one was open for 1% of the time, Pallas kernels for 0%

profile of v1, /device:TPU:1, one launch (start us, length us, event | category | flops | bytes accessed | tf_op | source)
XLA Modules:
  0.0 431.5 jit_solution(15466986259958730046)
XLA Ops:
  7.2 1.8 pad_maximum_fusion.1
  9.1 0.7 all-gather.5.cloned.1.call-update
  9.8 1.1 broadcast_in_dim.6
  10.9 81.3 %all_to_all.31 = bf16[32,8,4096]{2,1,0:T(8,128)(2,1)S(1)} all-to-all(bf16[32,8,4096]{2,1,0:T(8,128)(2,1)S(1)} %broadcast_in_dim.6), channel_id=1, replica_groups=mesh['list'=32,'shard'=16] {'list'}, dimensions={0} | all-to-all | bytes 4194304 | tf_op jit(solution)/shard_map/all_to_all | solution.py:26
  92.2 94.7 %all-gather.3.cloned.1.call-done = bf16[4096,688]{0,1:T(8,128)(2,1)} async-done(((bf16[256,688]{0,1:T(8,128)(2,1)}), bf16[4096,688]{0,1:T(8,128)(2,1)}) %all-gather.3.cloned.1.call-update) | async-done | bytes 5636112 | tf_op jit(solution)/shard_map/all_gather | solution.py:35
  186.9 2.9 fusion.9
  189.8 77.1 %all-gather.5.cloned.1.call-done = bf16[344,4096]{1,0:T(8,128)(2,1)} async-done(((bf16[344,256]{1,0:T(8,128)(2,1)}), bf16[344,4096]{1,0:T(8,128)(2,1)}) %all-gather.5.cloned.1.call-update) | async-done | bytes 2818064 | tf_op jit(solution)/shard_map/all_gather | solution.py:76
  266.9 7.7 %fusion = bf16[32,8,4096]{2,1,0:T(8,128)(2,1)} fusion(bf16[344,4096]{1,0:T(8,128)(2,1)} %all-gather.5.cloned.1.call-done, bf16[32,8,4096]{2,1,0:T(8,128)(2,1)S(1)} %all_to_all.31, bf16[4096,688]{0,1:T(8,128)(2,1)} %all-gather.3.cloned.1.call-done, f32[256,344]{0,1:T(8,128)S(1)} %fusion.9), kind=kOutput, calls=%fused_computation.1 | convolution fusion | flops 1444417536 | bytes 10182656 | tf_op jit(solution)/shard_map/dot_general | solution.py:74
  274.6 19.3 %all-to-all-start.1 = ((bf16[32,8,4096]{2,1,0:T(8,128)(2,1)}), bf16[32,8,4096]{2,1,0:T(8,128)(2,1)S(1)}, u32[]{:S(2)}, u32[]{:S(2)}) async-start(bf16[32,8,4096]{2,1,0:T(8,128)(2,1)} %fusion), calls=%async_computation.1 | async-start | bytes 4194304 | tf_op jit(solution)/shard_map/all_to_all | solution.py:49
  294.1 0.1 convert_element_type.84
  294.2 50.7 %all-to-all-done.1 = bf16[32,8,4096]{2,1,0:T(8,128)(2,1)S(1)} async-done(((bf16[32,8,4096]{2,1,0:T(8,128)(2,1)}), bf16[32,8,4096]{2,1,0:T(8,128)(2,1)S(1)}, u32[]{:S(2)}, u32[]{:S(2)}) %all-to-all-start.1) | async-done | bytes 2097184 | tf_op jit(solution)/shard_map/all_to_all | solution.py:49
  344.9 0.3 convert_reduce_fusion
  345.2 0.2 multiply_reduce_fusion
  345.5 0.7 convolution_convert_fusion.1
  346.2 0.3 concatenate.10
  346.5 0.5 pad_maximum_fusion
  347.1 23.8 %all_to_all.32 = bf16[32,2,4097]{2,1,0:T(2,128)(2,1)S(1)} all-to-all(bf16[32,2,4097]{2,1,0:T(2,128)(2,1)S(1)} %pad_maximum_fusion), channel_id=1, replica_groups=mesh['list'=32,'shard'=16] {'list'}, dimensions={0} | all-to-all | bytes 1048832 | tf_op jit(solution)/shard_map/all_to_all | solution.py:49
  370.9 0.4 reduce.1
  371.4 0.1 slice_reduce_fusion
  371.5 0.6 broadcast_in_dim.8
  372.1 5.5 %all-to-all-start.5 = ((bf16[16,1,2]{2,1,0:T(2,128)(2,1)}), bf16[16,1,2]{2,1,0:T(2,128)(2,1)S(1)}, u32[]{:S(2)}, u32[]{:S(2)}) async-start(bf16[16,1,2]{2,1,0:T(2,128)(2,1)} %broadcast_in_dim.8), calls=%async_computation.5 | async-start | bytes 16384 | tf_op jit(solution)/shard_map/all_to_all | solution.py:26
  377.6 7.3 %all-to-all-done.5 = bf16[16,1,2]{2,1,0:T(2,128)(2,1)S(1)} async-done(((bf16[16,1,2]{2,1,0:T(2,128)(2,1)}), bf16[16,1,2]{2,1,0:T(2,128)(2,1)S(1)}, u32[]{:S(2)}, u32[]{:S(2)}) %all-to-all-start.5) | async-done | bytes 96 | tf_op jit(solution)/shard_map/all_to_all | solution.py:26
  384.9 0.9 broadcast_in_dim.7
  385.8 3.5 all-to-all-start.4
  389.4 0.1 convert_reduce_fusion.2
  389.5 8.6 %all-to-all-done.4 = bf16[16,2,4096]{2,1,0:T(2,128)(2,1)S(1)} async-done(((bf16[16,2,4096]{2,1,0:T(2,128)(2,1)}), bf16[16,2,4096]{2,1,0:T(2,128)(2,1)S(1)}, u32[]{:S(2)}, u32[]{:S(2)}) %all-to-all-start.4) | async-done | bytes 262176 | tf_op jit(solution)/shard_map/all_to_all | solution.py:26
  398.1 0.2 convert_reduce_fusion.1
  398.4 0.7 add_divide_fusion
  399.1 0.5 stack.2
  399.5 24.0 %all_to_all.33 = bf16[32,2,4096]{2,1,0:T(2,128)(2,1)S(1)} all-to-all(bf16[32,2,4096]{2,1,0:T(2,128)(2,1)S(1)} %stack.2), channel_id=1, replica_groups=mesh['list'=32,'shard'=16] {'list'}, dimensions={0} | all-to-all | bytes 1048576 | tf_op jit(solution)/shard_map/all_to_all | solution.py:11
  423.6 0.2 reshape.55
  423.8 0.9 fusion.2
  (20 shorter events, 0.4 us)
Async XLA Ops:
  7.2 179.7 %all-gather.3.cloned.1.call-start = ((), (), s32[]{:S(2)}) async-start(), calls=%async_computation.6 | async-start | bytes 5988352 | tf_op jit(solution)/shard_map/all_gather | solution.py:35
  9.0 257.9 %all-gather.5.cloned.1.call-start = ((), (), s32[]{:S(2)}) async-start(), calls=%async_computation.7 | async-start | bytes 2994176 | tf_op jit(solution)/shard_map/all_gather | solution.py:76
  274.6 19.3 %copy-start.4 = (s32[8]{0:T(128)S(1)}, s32[8]{0:T(128)}, u32[]{:S(2)}) copy-start(s32[8]{0:T(128)} %param.15) | copy-start | bytes 100
  274.6 19.4 %copy-start.3 = (s32[8]{0:T(128)S(1)}, s32[8]{0:T(128)}, u32[]{:S(2)}) copy-start(s32[8]{0:T(128)} %param.14) | copy-start | bytes 100
  274.6 70.6 %copy-start = (bf16[8,4096]{1,0:T(8,128)(2,1)S(1)}, bf16[8,4096]{1,0:T(8,128)(2,1)}, u32[]{:S(2)}) copy-start(bf16[8,4096]{1,0:T(8,128)(2,1)} %param.8) | copy-start | bytes 196612
  274.6 70.8 %copy-start.2 = (f32[4096]{0:T(1024)S(1)}, f32[4096]{0:T(1024)}, u32[]{:S(2)}) copy-start(f32[4096]{0:T(1024)} %param.9) | copy-start | bytes 49156
  274.6 70.3 %all-to-all-start.1 = ((bf16[32,8,4096]{2,1,0:T(8,128)(2,1)}), bf16[32,8,4096]{2,1,0:T(8,128)(2,1)S(1)}, u32[]{:S(2)}, u32[]{:S(2)}) async-start(bf16[32,8,4096]{2,1,0:T(8,128)(2,1)} %fusion), calls=%async_computation.1 | async-start | bytes 4194304 | tf_op jit(solution)/shard_map/all_to_all | solution.py:49
  345.5 52.9 %copy-start.1 = (f32[2,4096]{1,0:T(2,128)S(1)}, f32[2,4096]{1,0:T(2,128)}, u32[]{:S(2)}) copy-start(f32[2,4096]{1,0:T(2,128)} %param.13) | copy-start | bytes 98308
  372.1 12.8 %all-to-all-start.5 = ((bf16[16,1,2]{2,1,0:T(2,128)(2,1)}), bf16[16,1,2]{2,1,0:T(2,128)(2,1)S(1)}, u32[]{:S(2)}, u32[]{:S(2)}) async-start(bf16[16,1,2]{2,1,0:T(2,128)(2,1)} %broadcast_in_dim.8), calls=%async_computation.5 | async-start | bytes 16384 | tf_op jit(solution)/shard_map/all_to_all | solution.py:26
  385.8 12.4 %all-to-all-start.4 = ((bf16[16,2,4096]{2,1,0:T(2,128)(2,1)}), bf16[16,2,4096]{2,1,0:T(2,128)(2,1)S(1)}, u32[]{:S(2)}, u32[]{:S(2)}) async-start(bf16[16,2,4096]{2,1,0:T(2,128)(2,1)} %broadcast_in_dim.7), calls=%async_computation.4 | async-start | bytes 524288 | tf_op jit(solution)/shard_map/all_to_all | solution.py:26
Sparse Core Ops, SparseCore 0:
  10.0 176.8 all-gather.2
  188.9 77.9 all-gather.4
